TPU v7x, 32 devices: a whole 2x2x4 slice. The times are simulated.
32 devices in a mesh: row: 8 (over y, x, core), col: 4 (over z).
Axes of the slice: x: 2, y: 2, z: 4, core: 2. Of those that a mesh axis runs over, the one named last changes fastest.
Arguments:
- a_matrix: float32 [2048, 2048], P('row', 'col'), may hold values from -0.9 to 0.9
- b_matrix: float32 [2048, 2048], P('row', 'col'), may hold values from -0.9 to 0.9
- a_panel: float32 [2048, 1024], P('row', 'col'), may hold values from -0.9 to 0.9
- b_panel: float32 [2048, 1024], P('row', 'col'), may hold values from -0.9 to 0.9
Outputs:
- triangle: float32 [1024, 1024], P('row', 'col')
- pencil_cross: float32 [2048, 2048], P('row', 'col')
All inputs are finite; a program needn't handle non-finite values.
Results may differ from a plain program's by a relative error of at most 0.0003.
Values sent between devices are 32-bit elements; how exact they have to be, the bound alone decides.
No kernel may reach another device: no remote copies, remote signals or barrier semaphores. Data moves between devices by JAX's collectives and lax.ppermute only.
A program may use at most 64 MiB of HBM per device.

v0:
```python
import jax
import jax.numpy as jnp
from jax import lax
from jax.sharding import PartitionSpec as P

HIGHEST = lax.Precision.HIGHEST


def local(a_matrix, b_matrix, a_panel, b_panel):
    row_count = a_matrix.shape[0]
    panel_width = a_panel.shape[1]
    full_a, full_pa, full_pb = (
        lax.all_gather(a_matrix, "col", axis=1, tiled=True),
        lax.all_gather(a_panel, "col", axis=1, tiled=True),
        lax.all_gather(b_panel, "col", axis=1, tiled=True),
    )
    stacked = jnp.concatenate([full_pb, -full_pa], 0)
    own_block = jnp.concatenate([b_panel, -a_panel], 0)
    partial_gram = jnp.dot(own_block.T, stacked, precision=HIGHEST)
    gram_rows = lax.psum(partial_gram, "row")
    gram_matrix = lax.all_gather(gram_rows, "col", axis=0, tiled=True)
    lower_factor = jnp.linalg.cholesky(gram_matrix)
    q_rows = jax.scipy.linalg.solve_triangular(lower_factor, stacked.T, lower=True).T
    upper_rows = q_rows[:row_count]
    lower_rows = q_rows[row_count:]
    row_index = lax.axis_index("row")
    col_index = lax.axis_index("col")
    tri_rows = gram_matrix.shape[0] // lax.axis_size("row")
    corner = lax.dynamic_slice(
        lower_factor, (col_index * panel_width, row_index * tri_rows), (panel_width, tri_rows)
    )
    triangle = corner.T
    partial_z = jnp.dot(lower_rows.T, b_matrix, precision=HIGHEST)
    z_columns = lax.psum(partial_z, "row")
    v_block = jnp.dot(upper_rows, z_columns, precision=HIGHEST)
    pencil_cross = lax.psum_scatter(
        -jnp.dot(full_a.T, v_block, precision=HIGHEST), "row", scatter_dimension=0, tiled=True
    )
    return (triangle, pencil_cross)


def solution(mesh):
    in_specs = (P("row", "col"), P("row", "col"), P("row", "col"), P("row", "col"))
    out_specs = (P("row", "col"), P("row", "col"))
    return jax.shard_map(local, mesh=mesh, in_specs=in_specs, out_specs=out_specs, check_vma=False)
```

profile of v0, /device:TPU:0, one launch (start us, length us, event | category | flops | bytes accessed | tf_op | source)
XLA Modules:
  0.0 741.9 jit_solution(5404969723252647219)
XLA Ops:
  9.7 30.6 %all-gather.7.cloned.1.call-done = f32[256,1024]{1,0:T(8,128)} async-done(((f32[256,256]{1,0:T(8,128)}), f32[256,1024]{1,0:T(8,128)}) %all-gather.7.cloned.1.call-update) | async-done | bytes 1048592 | tf_op jit(solution)/shard_map/all_gather | solution.py:14
  41.6 27.7 %all-gather.5.cloned.1.call-done = f32[256,1024]{1,0:T(8,128)} async-done(((f32[256,256]{1,0:T(8,128)}), f32[256,1024]{1,0:T(8,128)}) %all-gather.5.cloned.1.call-update) | async-done | bytes 1048592 | tf_op jit(solution)/shard_map/all_gather | solution.py:15
  75.1 56.2 %all-reduce.4.cloned.1.call-done = f32[256,1024]{0,1:T(8,128)} async-done(((f32[256,1024]{0,1:T(8,128)}), f32[256,1024]{0,1:T(8,128)}) %all-reduce.4.cloned.1.call-update) | async-done | bytes 1048592 | tf_op jit(solution)/shard_map/psum | solution.py:20
  132.9 79.8 %all-gather.9.cloned.1.call-done = f32[1024,1024]{0,1:T(8,128)} async-done(((f32[256,1024]{0,1:T(8,128)}), f32[1024,1024]{0,1:T(8,128)}) %all-gather.9.cloned.1.call-update) | async-done | bytes 4194320 | tf_op jit(solution)/shard_map/all_gather | solution.py:21
  224.6 11.7 %cholesky.223 = f32[128,128]{1,0:T(8,128)S(1)} custom-call(f32[128,128]{1,0:T(8,128)S(1)} %cholesky.580), custom_call_target="Cholesky" | custom-call | tf_op jit(solution)/shard_map/jit(cholesky)/cholesky | solution.py:22
  238.8 9.8 %custom-call.63 = f32[1,128,128]{1,2,0:T(8,128)S(1)} custom-call(f32[1,128,128]{2,1,0:T(8,128)S(1)} %get-tuple-element.70), custom_call_target="InvertDiagBlocksLowerTriangular" | custom-call | tf_op jit(solution)/shard_map/jit(cholesky)/cholesky | solution.py:22
  252.6 11.9 %cholesky.244 = f32[128,128]{1,0:T(8,128)S(1)} custom-call(f32[128,128]{1,0:T(8,128)S(1)} %cholesky.584), custom_call_target="Cholesky" | custom-call | tf_op jit(solution)/shard_map/jit(cholesky)/cholesky | solution.py:22
  265.1 9.8 %custom-call.64 = f32[1,128,128]{1,2,0:T(8,128)S(1)} custom-call(f32[1,128,128]{2,1,0:T(8,128)S(1)} %get-tuple-element.67), custom_call_target="InvertDiagBlocksLowerTriangular" | custom-call | tf_op jit(solution)/shard_map/jit(cholesky)/cholesky | solution.py:22
  278.3 11.7 %cholesky.468 = f32[128,128]{1,0:T(8,128)S(1)} custom-call(f32[128,128]{1,0:T(8,128)S(1)} %cholesky.589), custom_call_target="Cholesky" | custom-call | tf_op jit(solution)/shard_map/jit(cholesky)/cholesky | solution.py:22
  290.7 9.8 %custom-call.65 = f32[1,128,128]{1,2,0:T(8,128)S(1)} custom-call(f32[1,128,128]{2,1,0:T(8,128)S(1)} %get-tuple-element.64), custom_call_target="InvertDiagBlocksLowerTriangular" | custom-call | tf_op jit(solution)/shard_map/jit(cholesky)/cholesky | solution.py:22
  304.0 12.1 %cholesky.487 = f32[128,128]{1,0:T(8,128)S(1)} custom-call(f32[128,128]{1,0:T(8,128)S(1)} %cholesky.594), custom_call_target="Cholesky" | custom-call | tf_op jit(solution)/shard_map/jit(cholesky)/cholesky | solution.py:22
  316.7 9.8 %custom-call.66 = f32[1,128,128]{1,2,0:T(8,128)S(1)} custom-call(f32[1,128,128]{2,1,0:T(8,128)S(1)} %get-tuple-element.61), custom_call_target="InvertDiagBlocksLowerTriangular" | custom-call | tf_op jit(solution)/shard_map/jit(cholesky)/cholesky | solution.py:22
  330.0 11.7 %cholesky.506 = f32[128,128]{1,0:T(8,128)S(1)} custom-call(f32[128,128]{1,0:T(8,128)S(1)} %cholesky.599), custom_call_target="Cholesky" | custom-call | tf_op jit(solution)/shard_map/jit(cholesky)/cholesky | solution.py:22
  342.4 10.0 %custom-call.67 = f32[1,128,128]{1,2,0:T(8,128)S(1)} custom-call(f32[1,128,128]{2,1,0:T(8,128)S(1)} %get-tuple-element.58), custom_call_target="InvertDiagBlocksLowerTriangular" | custom-call | tf_op jit(solution)/shard_map/jit(cholesky)/cholesky | solution.py:22
  355.6 11.7 %cholesky.526 = f32[128,128]{1,0:T(8,128)S(1)} custom-call(f32[128,128]{1,0:T(8,128)S(1)} %cholesky.604), custom_call_target="Cholesky" | custom-call | tf_op jit(solution)/shard_map/jit(cholesky)/cholesky | solution.py:22
  368.0 9.8 %custom-call.68 = f32[1,128,128]{1,2,0:T(8,128)S(1)} custom-call(f32[1,128,128]{2,1,0:T(8,128)S(1)} %get-tuple-element.55), custom_call_target="InvertDiagBlocksLowerTriangular" | custom-call | tf_op jit(solution)/shard_map/jit(cholesky)/cholesky | solution.py:22
  380.8 11.7 %cholesky.546 = f32[128,128]{1,0:T(8,128)S(1)} custom-call(f32[128,128]{1,0:T(8,128)S(1)} %cholesky.609), custom_call_target="Cholesky" | custom-call | tf_op jit(solution)/shard_map/jit(cholesky)/cholesky | solution.py:22
  393.2 9.8 %custom-call.69 = f32[1,128,128]{1,2,0:T(8,128)S(1)} custom-call(f32[1,128,128]{2,1,0:T(8,128)S(1)} %get-tuple-element.52), custom_call_target="InvertDiagBlocksLowerTriangular" | custom-call | tf_op jit(solution)/shard_map/jit(cholesky)/cholesky | solution.py:22
  405.6 11.7 %cholesky.564 = f32[128,128]{1,0:T(8,128)S(1)} custom-call(f32[128,128]{1,0:T(8,128)S(1)} %convolution_subtract_fusion.13), custom_call_target="Cholesky" | custom-call | tf_op jit(solution)/shard_map/jit(cholesky)/cholesky | solution.py:22
  434.3 27.5 %while.1 = (s32[]{:T(128)}, f32[1024,1024]{1,0:T(8,128)}, s32[8,2]{0,1:T(2,128)S(1)}, f32[8,128,128]{2,1,0:T(8,128)}, s32[]{:T(128)}) while((s32[]{:T(128)}, f32[1024,1024]{1,0:T(8,128)}, s32[8,2]{0,1:T(2,128)S(1)}, f32[8,128,128]{2,1,0:T(8,128)}, s32[]{:T(128)}) %tuple.63), condition=%wide.while_cond, body=%wide.while_body.sunk | while | flops 2 | bytes 132205 | solution.py:23
  461.8 79.8 %custom-call.70 = f32[8,128,128]{1,2,0:T(8,128)S(1)} custom-call(f32[8,128,128]{2,1,0:T(8,128)} %get-tuple-element.9), custom_call_target="InvertDiagBlocksLowerTriangular" | custom-call | tf_op jit(solution)/shard_map/jit(_solve_triangular)/triangular_solve | solution.py:23
  570.1 59.8 %all-reduce.6.cloned.1.call-done = f32[1024,512]{1,0:T(8,128)} async-done(((f32[1024,512]{1,0:T(8,128)}), f32[1024,512]{1,0:T(8,128)}) %all-reduce.6.cloned.1.call-update) | async-done | bytes 2097168 | tf_op jit(solution)/shard_map/psum | solution.py:34
  633.4 42.7 %all-gather.11.cloned.1.call-done = f32[256,2048]{1,0:T(8,128)} async-done(((f32[256,512]{1,0:T(8,128)}), f32[256,2048]{1,0:T(8,128)}) %all-gather.11.cloned.1.call-update) | async-done | bytes 2097168 | tf_op jit(solution)/shard_map/all_gather | solution.py:13
  684.5 48.3 %reduce-scatter.2.cloned.1.call-done = f32[256,512]{0,1:T(8,128)} async-done(((f32[2048,512]{0,1:T(8,128)}), f32[256,512]{0,1:T(8,128)}) %reduce-scatter.2.cloned.1.call-update) | async-done | bytes 524304 | tf_op jit(solution)/shard_map/reduce_scatter | solution.py:36
  (120 shorter events, 134.3 us)
Async XLA Ops:
  7.2 559.1 %copy-start = (f32[256,512]{1,0:T(8,128)S(1)}, f32[256,512]{1,0:T(8,128)}, u32[]{:S(2)}) copy-start(f32[256,512]{1,0:T(8,128)} %param.5) | copy-start | bytes 1572868
  7.2 62.1 %copy-start.6 = (f32[256,256]{1,0:T(8,128)S(1)}, f32[256,256]{1,0:T(8,128)}, u32[]{:S(2)}) copy-start(f32[256,256]{1,0:T(8,128)} %param.7) | copy-start | bytes 786436
  7.2 33.1 %all-gather.7.cloned.1.call-start = ((), (), s32[]{:S(2)}) async-start(), calls=%async_computation.2 | async-start | bytes 1310720 | tf_op jit(solution)/shard_map/all_gather | solution.py:14
  7.9 61.3 %all-gather.5.cloned.1.call-start = ((), (), s32[]{:S(2)}) async-start(), calls=%async_computation.1 | async-start | bytes 1310720 | tf_op jit(solution)/shard_map/all_gather | solution.py:15
  8.7 122.6 %all-reduce.4.cloned.1.call-start = ((), (), s32[]{:S(2)}) async-start(), calls=%async_computation.3 | async-start | bytes 2097152 | tf_op jit(solution)/shard_map/psum | solution.py:20
  69.3 62.1 %copy-start.3 = (f32[256,1024]{1,0:T(8,128)S(1)}, f32[256,1024]{1,0:T(8,128)}, u32[]{:S(2)}) copy-start(f32[256,1024]{1,0:T(8,128)} %all-gather.5.cloned.1.call-done) | copy-start | bytes 3145732
  75.0 137.7 %all-gather.9.cloned.1.call-start = ((), (), s32[]{:S(2)}) async-start(), calls=%async_computation.4 | async-start | bytes 5242880 | tf_op jit(solution)/shard_map/all_gather | solution.py:21
  131.3 498.5 %all-reduce.6.cloned.1.call-start = ((), (), s32[]{:S(2)}) async-start(), calls=%async_computation.5 | async-start | bytes 4194304 | tf_op jit(solution)/shard_map/psum | solution.py:34
  222.7 1.9 copy-start.1
  427.6 114.1 %copy-start.2 = (f32[1024,512]{0,1:T(8,128)S(1)}, f32[1024,512]{0,1:T(8,128)}, u32[]{:S(2)}) copy-start(f32[1024,512]{0,1:T(8,128)} %fusion.2) | copy-start | bytes 6291460
  565.0 1.3 copy-start.4
  569.4 60.4 %copy-start.5 = (f32[1024,512]{1,0:T(8,128)S(1)}, f32[1024,512]{1,0:T(8,128)}, u32[]{:S(2)}) copy-start(f32[1024,512]{1,0:T(8,128)} %copy-done.4) | copy-start | bytes 6291460
  569.4 106.6 %all-gather.11.cloned.1.call-start = ((), (), s32[]{:S(2)}) async-start(), calls=%async_computation.6 | async-start | bytes 2621440 | tf_op jit(solution)/shard_map/all_gather | solution.py:13
  570.0 162.8 %reduce-scatter.2.cloned.1.call-start = ((), (), s32[]{:S(2)}) async-start(), calls=%async_computation.7 | async-start | bytes 4718592 | tf_op jit(solution)/shard_map/reduce_scatter | solution.py:36
Sparse Core Ops, SparseCore 0:
  9.6 30.6 all-gather.6
  41.9 27.3 all-gather.4
  75.2 56.0 all-reduce.3
  132.7 79.9 all-gather.8
  569.6 60.2 all-reduce.5
  631.3 44.7 all-gather.10
  682.9 49.8 reduce-scatter.1
where the time goes:
time: 747 us; the launch traced here: 742 us
  waiting for transfers between devices  347 us (46%)
  other arithmetic  267 us (36%)
  matrix products  65.4 us (9%)
  local copies, waits for them, and re-layouts  42.5 us (6%)
  between operations  19.6 us (3%)
    another operation x30, other arithmetic, local(): lower_factor = jnp.linalg.cholesky(gram_matrix)  172 us
    another operation x3, other arithmetic, local(): jax.scipy.linalg.solve_triangular(lower_factor, stacked.T, lower=True)  86.6 us
    all_gather x1, waiting for transfers between devices, local(): gram_matrix = lax.all_gather(gram_rows, 'col', axis=0, tiled=True)  79.8 us
    psum x1, waiting for transfers between devices, local(): z_columns = lax.psum(partial_z, 'row')  59.8 us
    psum x1, waiting for transfers between devices, local(): gram_rows = lax.psum(partial_gram, 'row')  56.2 us
    reduce_scatter x1, waiting for transfers between devices, local(): lax.psum_scatter(-jnp.dot(full_a.T, v_block, precision=HIGHEST), 'row', s...  48.3 us
    all_gather x1, waiting for transfers between devices, local(): lax.all_gather(a_matrix, 'col', axis=1, tiled=True)  42.7 us
    all_gather x1, waiting for transfers between devices, local(): lax.all_gather(a_panel, 'col', axis=1, tiled=True)  30.6 us
  transfers between devices with their start and end apart: 7, of which 7 were waited for; matrix products, arithmetic and copies ran while one was open for 1% of the time, Pallas kernels for 0%

commit v1 on v0

--- a/solution.py
+++ b/solution.py
@@ -6,11 +6,32 @@
 HIGHEST = lax.Precision.HIGHEST
 
 
+def ring_gather(x, axis, dim):
+    size, place, rows = (lax.axis_size(axis), lax.axis_index(axis), x.shape[dim])
+    upward = [(i, (i + 1) % size) for i in range(size)]
+    left = [(i, (i - 1) % size) for i in range(size)]
+    result = jnp.zeros((*x.shape[:dim], size * rows, *x.shape[dim + 1 :]), x.dtype)
+    result = lax.dynamic_update_slice_in_dim(result, x, place * rows, axis=dim)
+    from_left = from_right = x
+    half = size // 2
+    for lap in range(1, half + 1):
+        from_left = lax.ppermute(from_left, axis, upward)
+        result = lax.dynamic_update_slice_in_dim(
+            result, from_left, (place - lap) % size * rows, axis=dim
+        )
+        if lap < size - half:
+            from_right = lax.ppermute(from_right, axis, left)
+            result = lax.dynamic_update_slice_in_dim(
+                result, from_right, (place + lap) % size * rows, axis=dim
+            )
+    return result
+
+
 def local(a_matrix, b_matrix, a_panel, b_panel):
     row_count = a_matrix.shape[0]
     panel_width = a_panel.shape[1]
     full_a, full_pa, full_pb = (
-        lax.all_gather(a_matrix, "col", axis=1, tiled=True),
+        ring_gather(a_matrix, "col", 1),
         lax.all_gather(a_panel, "col", axis=1, tiled=True),
         lax.all_gather(b_panel, "col", axis=1, tiled=True),
     )

time: 747 us -> 702 us (0.940)
  waiting for transfers between devices: 347 us -> 298 us
    all_gather x1 -> x0, waiting for transfers between devices: 42.7 us -> none  [local(): lax.all_gather(a_matrix, 'col', axis=1, tiled=True)]
    psum x1, waiting for transfers between devices: 59.8 us -> 32 us  [local(): z_columns = lax.psum(partial_z, 'row')]
    ppermute x0 -> x3, waiting for transfers between devices: none -> 21.6 us  [the longest x1 21.6 us: ring_gather(): from_right = lax.ppermute(from_right, axis, left)]
  transfers between devices with their start and end apart: 7 -> 9, of which waited for: 7 -> 7; matrix products, arithmetic and copies ran while one was open for 1% -> 51% of each run, Pallas kernels for 0% -> 0%
where the time goes in v1:
time: 702 us; the launch traced here: 697 us
  waiting for transfers between devices  298 us (42%)
  other arithmetic  267 us (38%)
  matrix products  64.2 us (9%)
  local copies, waits for them, and re-layouts  44.1 us (6%)
  between operations  19.7 us (3%)
    another operation x30, other arithmetic, local(): lower_factor = jnp.linalg.cholesky(gram_matrix)  172 us
    another operation x3, other arithmetic, local(): jax.scipy.linalg.solve_triangular(lower_factor, stacked.T, lower=True)  86.6 us
    all_gather x1, waiting for transfers between devices, local(): gram_matrix = lax.all_gather(gram_rows, 'col', axis=0, tiled=True)  80.1 us
    psum x1, waiting for transfers between devices, local(): gram_rows = lax.psum(partial_gram, 'row')  56.2 us
    reduce_scatter x1, waiting for transfers between devices, local(): lax.psum_scatter(-jnp.dot(full_a.T, v_block, precision=HIGHEST), 'row', s...  48.7 us
    psum x1, waiting for transfers between devices, local(): z_columns = lax.psum(partial_z, 'row')  32 us
    all_gather x1, waiting for transfers between devices, local(): lax.all_gather(a_panel, 'col', axis=1, tiled=True)  30.6 us
    all_gather x1, waiting for transfers between devices, local(): lax.all_gather(b_panel, 'col', axis=1, tiled=True)  27.7 us
  transfers between devices with their start and end apart: 9, of which 7 were waited for; matrix products, arithmetic and copies ran while one was open for 51% of the time, Pallas kernels for 0%

profile of v1, /device:TPU:0, one launch (start us, length us, event | category | flops | bytes accessed | tf_op | source)
XLA Modules:
  0.0 697.3 jit_solution(10578782999233248892)
XLA Ops:
  9.7 30.6 %all-gather.6.cloned.1.call-done = f32[256,1024]{1,0:T(8,128)} async-done(((f32[256,256]{1,0:T(8,128)}), f32[256,1024]{1,0:T(8,128)}) %all-gather.6.cloned.1.call-update) | async-done | bytes 1048592 | tf_op jit(solution)/shard_map/all_gather | solution.py:35
  41.6 27.7 %all-gather.4.cloned.1.call-done = f32[256,1024]{1,0:T(8,128)} async-done(((f32[256,256]{1,0:T(8,128)}), f32[256,1024]{1,0:T(8,128)}) %all-gather.4.cloned.1.call-update) | async-done | bytes 1048592 | tf_op jit(solution)/shard_map/all_gather | solution.py:36
  75.1 56.2 %all-reduce.4.cloned.1.call-done = f32[256,1024]{0,1:T(8,128)} async-done(((f32[256,1024]{0,1:T(8,128)}), f32[256,1024]{0,1:T(8,128)}) %all-reduce.4.cloned.1.call-update) | async-done | bytes 1048592 | tf_op jit(solution)/shard_map/psum | solution.py:41
  134.3 80.1 %all-gather.8.cloned.1.call-done = f32[1024,1024]{0,1:T(8,128)} async-done(((f32[256,1024]{0,1:T(8,128)}), f32[1024,1024]{0,1:T(8,128)}) %all-gather.8.cloned.1.call-update) | async-done | bytes 4194320 | tf_op jit(solution)/shard_map/all_gather | solution.py:42
  226.3 11.7 %cholesky.223 = f32[128,128]{1,0:T(8,128)S(1)} custom-call(f32[128,128]{1,0:T(8,128)S(1)} %cholesky.580), custom_call_target="Cholesky" | custom-call | tf_op jit(solution)/shard_map/jit(cholesky)/cholesky | solution.py:43
  238.1 9.8 %custom-call.63 = f32[1,128,128]{1,2,0:T(8,128)S(1)} custom-call(f32[1,128,128]{2,1,0:T(8,128)S(1)} %get-tuple-element.70), custom_call_target="InvertDiagBlocksLowerTriangular" | custom-call | tf_op jit(solution)/shard_map/jit(cholesky)/cholesky | solution.py:43
  254.3 11.9 %cholesky.244 = f32[128,128]{1,0:T(8,128)S(1)} custom-call(f32[128,128]{1,0:T(8,128)S(1)} %cholesky.584), custom_call_target="Cholesky" | custom-call | tf_op jit(solution)/shard_map/jit(cholesky)/cholesky | solution.py:43
  266.8 9.8 %custom-call.64 = f32[1,128,128]{1,2,0:T(8,128)S(1)} custom-call(f32[1,128,128]{2,1,0:T(8,128)S(1)} %get-tuple-element.67), custom_call_target="InvertDiagBlocksLowerTriangular" | custom-call | tf_op jit(solution)/shard_map/jit(cholesky)/cholesky | solution.py:43
  280.0 11.7 %cholesky.468 = f32[128,128]{1,0:T(8,128)S(1)} custom-call(f32[128,128]{1,0:T(8,128)S(1)} %cholesky.589), custom_call_target="Cholesky" | custom-call | tf_op jit(solution)/shard_map/jit(cholesky)/cholesky | solution.py:43
  293.0 9.8 %custom-call.65 = f32[1,128,128]{1,2,0:T(8,128)S(1)} custom-call(f32[1,128,128]{2,1,0:T(8,128)S(1)} %get-tuple-element.64), custom_call_target="InvertDiagBlocksLowerTriangular" | custom-call | tf_op jit(solution)/shard_map/jit(cholesky)/cholesky | solution.py:43
  306.4 12.1 %cholesky.487 = f32[128,128]{1,0:T(8,128)S(1)} custom-call(f32[128,128]{1,0:T(8,128)S(1)} %cholesky.594), custom_call_target="Cholesky" | custom-call | tf_op jit(solution)/shard_map/jit(cholesky)/cholesky | solution.py:43
  319.8 9.8 %custom-call.66 = f32[1,128,128]{1,2,0:T(8,128)S(1)} custom-call(f32[1,128,128]{2,1,0:T(8,128)S(1)} %get-tuple-element.61), custom_call_target="InvertDiagBlocksLowerTriangular" | custom-call | tf_op jit(solution)/shard_map/jit(cholesky)/cholesky | solution.py:43
  333.0 11.7 %cholesky.506 = f32[128,128]{1,0:T(8,128)S(1)} custom-call(f32[128,128]{1,0:T(8,128)S(1)} %cholesky.599), custom_call_target="Cholesky" | custom-call | tf_op jit(solution)/shard_map/jit(cholesky)/cholesky | solution.py:43
  346.1 9.9 %custom-call.67 = f32[1,128,128]{1,2,0:T(8,128)S(1)} custom-call(f32[1,128,128]{2,1,0:T(8,128)S(1)} %get-tuple-element.58), custom_call_target="InvertDiagBlocksLowerTriangular" | custom-call | tf_op jit(solution)/shard_map/jit(cholesky)/cholesky | solution.py:43
  359.4 11.7 %cholesky.526 = f32[128,128]{1,0:T(8,128)S(1)} custom-call(f32[128,128]{1,0:T(8,128)S(1)} %cholesky.604), custom_call_target="Cholesky" | custom-call | tf_op jit(solution)/shard_map/jit(cholesky)/cholesky | solution.py:43
  372.4 9.8 %custom-call.68 = f32[1,128,128]{1,2,0:T(8,128)S(1)} custom-call(f32[1,128,128]{2,1,0:T(8,128)S(1)} %get-tuple-element.55), custom_call_target="InvertDiagBlocksLowerTriangular" | custom-call | tf_op jit(solution)/shard_map/jit(cholesky)/cholesky | solution.py:43
  385.2 11.9 %cholesky.546 = f32[128,128]{1,0:T(8,128)S(1)} custom-call(f32[128,128]{1,0:T(8,128)S(1)} %cholesky.609), custom_call_target="Cholesky" | custom-call | tf_op jit(solution)/shard_map/jit(cholesky)/cholesky | solution.py:43
  398.3 9.8 %custom-call.69 = f32[1,128,128]{1,2,0:T(8,128)S(1)} custom-call(f32[1,128,128]{2,1,0:T(8,128)S(1)} %get-tuple-element.52), custom_call_target="InvertDiagBlocksLowerTriangular" | custom-call | tf_op jit(solution)/shard_map/jit(cholesky)/cholesky | solution.py:43
  410.8 11.7 %cholesky.564 = f32[128,128]{1,0:T(8,128)S(1)} custom-call(f32[128,128]{1,0:T(8,128)S(1)} %convolution_subtract_fusion.13), custom_call_target="Cholesky" | custom-call | tf_op jit(solution)/shard_map/jit(cholesky)/cholesky | solution.py:43
  436.2 27.5 %while.1 = (s32[]{:T(128)}, f32[1024,1024]{1,0:T(8,128)}, s32[8,2]{0,1:T(2,128)S(1)}, f32[8,128,128]{2,1,0:T(8,128)}, s32[]{:T(128)}) while((s32[]{:T(128)}, f32[1024,1024]{1,0:T(8,128)}, s32[8,2]{0,1:T(2,128)S(1)}, f32[8,128,128]{2,1,0:T(8,128)}, s32[]{:T(128)}) %tuple.63), condition=%wide.while_cond, body=%wide.while_body.sunk | while | flops 2 | bytes 132205 | solution.py:44
  463.7 79.8 %custom-call.70 = f32[8,128,128]{1,2,0:T(8,128)S(1)} custom-call(f32[8,128,128]{2,1,0:T(8,128)} %get-tuple-element.9), custom_call_target="InvertDiagBlocksLowerTriangular" | custom-call | tf_op jit(solution)/shard_map/jit(_solve_triangular)/triangular_solve | solution.py:44
  575.1 21.6 %collective-permute-done.1 = f32[256,512]{1,0:T(8,128)} collective-permute-done((f32[256,512]{1,0:T(8,128)S(1)}, f32[256,512]{1,0:T(8,128)}, u32[]{:S(2)}, u32[]{:S(2)}) %collective-permute-start.1) | collective-permute-done | bytes 524320 | tf_op jit(solution)/shard_map/ppermute | solution.py:23
  598.9 32.0 %all-reduce.6.cloned.1.call-done = f32[1024,512]{1,0:T(8,128)} async-done(((f32[1024,512]{1,0:T(8,128)}), f32[1024,512]{1,0:T(8,128)}) %all-reduce.6.cloned.1.call-update) | async-done | bytes 2097168 | tf_op jit(solution)/shard_map/psum | solution.py:55
  641.6 48.7 %reduce-scatter.2.cloned.1.call-done = f32[256,512]{1,0:T(8,128)} async-done(((f32[2048,512]{1,0:T(8,128)}), f32[256,512]{1,0:T(8,128)}) %reduce-scatter.2.cloned.1.call-update) | async-done | bytes 524304 | tf_op jit(solution)/shard_map/reduce_scatter | solution.py:57
  (127 shorter events, 137.7 us)
Async XLA Ops:
  7.2 561.0 %copy-start = (f32[256,512]{1,0:T(8,128)S(1)}, f32[256,512]{1,0:T(8,128)}, u32[]{:S(2)}) copy-start(f32[256,512]{1,0:T(8,128)} %param.5) | copy-start | bytes 1572868
  7.2 62.1 %copy-start.5 = (f32[256,256]{1,0:T(8,128)S(1)}, f32[256,256]{1,0:T(8,128)}, u32[]{:S(2)}) copy-start(f32[256,256]{1,0:T(8,128)} %param.7) | copy-start | bytes 786436
  7.2 33.1 %all-gather.6.cloned.1.call-start = ((), (), s32[]{:S(2)}) async-start(), calls=%async_computation.2 | async-start | bytes 1310720 | tf_op jit(solution)/shard_map/all_gather | solution.py:35
  7.9 61.3 %all-gather.4.cloned.1.call-start = ((), (), s32[]{:S(2)}) async-start(), calls=%async_computation.1 | async-start | bytes 1310720 | tf_op jit(solution)/shard_map/all_gather | solution.py:36
  8.7 122.6 %all-reduce.4.cloned.1.call-start = ((), (), s32[]{:S(2)}) async-start(), calls=%async_computation.3 | async-start | bytes 2097152 | tf_op jit(solution)/shard_map/psum | solution.py:41
  69.3 63.6 %copy-start.3 = (f32[256,1024]{1,0:T(8,128)S(1)}, f32[256,1024]{1,0:T(8,128)}, u32[]{:S(2)}) copy-start(f32[256,1024]{1,0:T(8,128)} %all-gather.4.cloned.1.call-done) | copy-start | bytes 3145732
  75.0 139.4 %all-gather.8.cloned.1.call-start = ((), (), s32[]{:S(2)}) async-start(), calls=%async_computation.4 | async-start | bytes 5242880 | tf_op jit(solution)/shard_map/all_gather | solution.py:42
  131.3 499.7 %all-reduce.6.cloned.1.call-start = ((), (), s32[]{:S(2)}) async-start(), calls=%async_computation.5 | async-start | bytes 4194304 | tf_op jit(solution)/shard_map/psum | solution.py:55
  131.3 441.6 %collective-permute-start = (f32[256,512]{1,0:T(8,128)}, f32[256,512]{1,0:T(8,128)}, u32[]{:S(2)}, u32[]{:S(2)}) collective-permute-start(f32[256,512]{1,0:T(8,128)} %param.4), channel_id=1, source_target_pairs={{0,1},{1,2},{2,3},{3,0},{4,5},{5,6},{6,7},{7,4},{8,9},{9,10},{10,1... | collective-permute-start | bytes 1572872 | tf_op jit(solution)/shard_map/ppermute | solution.py:18
  224.4 1.9 copy-start.1
  429.5 114.1 %copy-start.2 = (f32[1024,512]{0,1:T(8,128)S(1)}, f32[1024,512]{0,1:T(8,128)}, u32[]{:S(2)}) copy-start(f32[1024,512]{0,1:T(8,128)} %fusion.2) | copy-start | bytes 6291460
  566.9 1.3 copy-start.4
  568.2 3.3 copy-start.6
  571.4 118.9 %reduce-scatter.2.cloned.1.call-start = ((), (), s32[]{:S(2)}) async-start(), calls=%async_computation.6 | async-start | bytes 4718592 | tf_op jit(solution)/shard_map/reduce_scatter | solution.py:57
  571.5 25.2 %collective-permute-start.1 = (f32[256,512]{1,0:T(8,128)S(1)}, f32[256,512]{1,0:T(8,128)}, u32[]{:S(2)}, u32[]{:S(2)}) collective-permute-start(f32[256,512]{1,0:T(8,128)S(1)} %copy-done.6), channel_id=1, source_target_pairs={{0,3},{1,0},{2,1},{3,2},{4,7},{5,4},{6,5},{7,6},{8,11},{9,8},{10,9... | collective-permute-start | bytes 1572872 | tf_op jit(solution)/shard_map/ppermute | solution.py:23
  573.0 24.8 %collective-permute-start.2 = (f32[256,512]{1,0:T(8,128)}, f32[256,512]{1,0:T(8,128)}, u32[]{:S(2)}, u32[]{:S(2)}) collective-permute-start(f32[256,512]{1,0:T(8,128)} %collective-permute-done), channel_id=1, source_target_pairs={{0,1},{1,2},{2,3},{3,0},{4,5},{5,6},{6,7},{7,4},{8,9},{9,10},{10,1... | collective-permute-start | bytes 1572872 | tf_op jit(solution)/shard_map/ppermute | solution.py:18
Sparse Core Ops, SparseCore 0:
  9.6 30.6 all-gather.5
  41.9 27.3 all-gather.3
  75.2 56.0 all-reduce.3
  132.7 81.6 all-gather.7
  571.6 59.3 all-reduce.5
  640.0 50.2 reduce-scatter.1
